TPU v7x, 128 devices: a whole 4x4x4 slice. The times are simulated.
128 devices in a mesh: sec: 2 (over z_lo), tile: 64 (over y, z_hi, x, core).
Axes of the slice: x: 4, y: 4, z: 4 (z_hi: 2, z_lo: 2; z = z_hi * 2 + z_lo), core: 2. Of those that a mesh axis runs over, the one named last changes fastest.
Arguments:
- atmosphere: bfloat16 [128, 360, 384], P(('sec', 'tile')), may hold values from -6 to 6
- ocean_state: bfloat16 [512, 1440, 128], P('tile', 'sec'), may hold values from -6 to 6
- land_mask: int32 [512, 1440], P('tile', 'sec'), may hold values 0 or 1
- crossing_bands: int32 [64, 4], P('tile'), may hold values from 0 to 127, as said below
- ocean_regrid: float32 [64, 4, 8, 1], P('tile'), may hold values from 0 to 1, as said below
- atmosphere_regrid: float32 [64, 4, 1, 8], P('tile'), may hold values from 0 to 1, as said below
- surface_read: bfloat16 [128], replicated, may hold values from -0.5 to 0.5
- surface_embed: float32 [384], replicated, may hold values from -4 to 4
- flux_read: bfloat16 [384, 8], replicated, may hold values from -0.3125 to 0.3125
- flux_embed: bfloat16 [8, 128], replicated, may hold values from -2 to 2
- legendre_forward: bfloat16 [128, 128, 128], P(('sec', 'tile')), may hold values from -0.5 to 0.5
- legendre_inverse: bfloat16 [128, 128, 128], P(('sec', 'tile')), may hold values from -0.5 to 0.5
- spectral_mix: bfloat16 [2, 384, 384], replicated, may hold values from -0.3125 to 0.3125
- conv_kernel: bfloat16 [2, 7, 7, 128], replicated, may hold values from -0.875 to 0.875
- norm_gain: float32 [2, 128], replicated, may hold values from 0.1 to 1.9
- expand_weight: bfloat16 [2, 128, 512], replicated, may hold values from -0.5 to 0.5
- project_weight: bfloat16 [2, 512, 128], replicated, may hold values from -0.25 to 0.25
- atmosphere_cotangent: bfloat16 [128, 360, 384], P(('sec', 'tile')), may hold values from -6 to 6
- ocean_cotangent: bfloat16 [512, 1440, 128], P('tile', 'sec'), may hold values from -6 to 6
Outputs:
- atmosphere_next: bfloat16 [128, 360, 384], P(('sec', 'tile'))
- ocean_next: bfloat16 [512, 1440, 128], P('tile', 'sec')
- atmosphere_grad: float32 [128, 360, 384], P(('sec', 'tile'))
- ocean_grad: float32 [512, 1440, 128], P('tile', 'sec')
Inputs may be any that keep to these rules, and one draw needn't show every extreme that they name: `crossing_bands`: row j lists between 1 and 4 consecutive distinct atmosphere bands, then repeats its last band; some row lists 4. Its first band is j * 2 - 1, j * 2 or j * 2 + 1, raised to 0 or lowered as far as needed for the list to end at band 128 - 1 at most. `ocean_regrid`: zero in the repeated slots of crossing_bands; the entries of each ocean row sum to one. `atmosphere_regrid`: zero in the repeated slots of crossing_bands.
All inputs are finite; a program needn't handle non-finite values. No bound on the sum of `land_mask` on one device may be relied on, other than what follows from the above.
Results may differ from a plain program's by a relative error of at most 0.008.
Values may be sent and summed in bfloat16 or wider, within the bound.
A program may use at most 128 MiB of HBM per device.

v0:
```python
import jax
import jax.numpy as jnp
from jax import lax
from jax.sharding import Mesh
from jax.sharding import PartitionSpec as P

SEC_TILE = ("sec", "tile_0", "tile_1", "tile_2", "tile_3")
TILE = ("tile_0", "tile_1", "tile_2", "tile_3")


def in_blocks(x, dim, size):
    lengths = x.shape
    blocks = x.reshape(*lengths[:dim], size, lengths[dim] // size, *lengths[dim + 1 :])
    return jnp.moveaxis(blocks, dim, 0)


def laid_out(blocks, dim):
    lengths = list(blocks.shape[1:])
    lengths[dim] *= blocks.shape[0]
    return jnp.moveaxis(blocks, 0, dim).reshape(lengths)


def turned_blocks(blocks, axes, sequence):
    lengths = [lax.axis_size(a) for a in axes]
    blocks = blocks.reshape(*lengths, *blocks.shape[1:])
    for k in sequence:
        blocks = lax.all_to_all(blocks, axes[k], split_axis=k, concat_axis=k, tiled=True)
    return blocks.reshape(-1, *blocks.shape[len(axes) :])


def two_step_exchange(x, groups, sequence, split_dim, concat_dim):
    size = lax.axis_size(groups[0]) * lax.axis_size(groups[1])
    blocks = in_blocks(x, split_dim, size)
    return laid_out(turned_blocks(blocks, groups, sequence), concat_dim)


def with_halo(x, sides, width, wrap):
    for axis, dim in sides:
        size, length = (lax.axis_size(axis), x.shape[dim])
        up = [(i, (i + 1) % size) for i in range(size if wrap else size - 1)]
        down = [(j, i) for i, j in up]
        last = lax.slice_in_dim(x, length - width, length, axis=dim)
        first = lax.slice_in_dim(x, 0, width, axis=dim)
        before = lax.ppermute(last, axis, up)
        after = lax.ppermute(first, axis, down)
        x = jnp.concatenate([before, x, after], axis=dim)
    return x


def wave_table(lon_count, mode_count):
    longitude = jnp.arange(lon_count, dtype=jnp.int32)
    wavenumber = jnp.arange(mode_count, dtype=jnp.int32)
    phase = (longitude[:, None] * wavenumber[None, :] % lon_count).astype(jnp.float32) * (
        2.0 * jnp.pi / lon_count
    )
    scaled = jnp.stack([jnp.cos(phase), -jnp.sin(phase)], axis=2) * jnp.sqrt(
        jnp.float32(2.0 / lon_count)
    )
    return scaled.reshape(lon_count, 2 * mode_count).astype(jnp.bfloat16)


def depthwise(window, kernel):
    radius = kernel.shape[0] // 2
    height = window.shape[0] - 2 * radius
    extent = window.shape[1] - 2 * radius
    wide = window.astype(jnp.float32)
    weights = kernel.astype(jnp.float32)
    total = jnp.zeros((height, extent, window.shape[2]), jnp.float32)
    for shift_row in range(kernel.shape[0]):
        for shift_col in range(kernel.shape[1]):
            total = (
                total
                + wide[shift_row : shift_row + height, shift_col : shift_col + extent]
                * weights[shift_row, shift_col]
            )
    return total


def cell_forward(hidden, gain, expand, project):
    center = hidden - jnp.mean(hidden, axis=-1, keepdims=True)
    inverse_std = lax.rsqrt(jnp.mean(center * center, axis=-1, keepdims=True) + 1e-06)
    normed = (center * inverse_std * gain).astype(jnp.bfloat16)
    before = jnp.dot(normed, expand, preferred_element_type=jnp.float32)
    active = jax.nn.gelu(before).astype(jnp.bfloat16)
    return jnp.dot(active, project, preferred_element_type=jnp.float32)


def cell_backward(hidden, gain, expand, project, mask_value, cotangent):
    center = hidden - jnp.mean(hidden, axis=-1, keepdims=True)
    inverse_std = lax.rsqrt(jnp.mean(center * center, axis=-1, keepdims=True) + 1e-06)
    unit = center * inverse_std
    normed = (unit * gain).astype(jnp.bfloat16)
    before = jnp.dot(normed, expand, preferred_element_type=jnp.float32)
    masked = (mask_value[:, :, None] * cotangent).astype(jnp.bfloat16)
    active_adjoint = jnp.dot(masked, project.T, preferred_element_type=jnp.float32)
    _, gelu_back = jax.vjp(jax.nn.gelu, before)
    before_adjoint = gelu_back(active_adjoint)[0].astype(jnp.bfloat16)
    normed_adjoint = jnp.dot(before_adjoint, expand.T, preferred_element_type=jnp.float32)
    scaled = normed_adjoint * gain
    result = inverse_std * (
        scaled
        - jnp.mean(scaled, axis=-1, keepdims=True)
        - unit * jnp.mean(scaled * unit, axis=-1, keepdims=True)
    )
    return result.astype(jnp.bfloat16)


def ocean_matrix(bands_row, blocks, lat_count):
    lat_band = blocks.shape[2]
    index = bands_row[:, None] * lat_band + jnp.arange(lat_band, dtype=jnp.int32)[None, :]
    onehot = (index[:, :, None] == jnp.arange(lat_count, dtype=jnp.int32)[None, None, :]).astype(
        jnp.float32
    )
    return jnp.einsum("poi,pia->oa", blocks, onehot, precision=lax.Precision.HIGHEST)


def atmosphere_matrix(bands_row, blocks, lat_count):
    lat_band = blocks.shape[1]
    index = bands_row[:, None] * lat_band + jnp.arange(lat_band, dtype=jnp.int32)[None, :]
    onehot = (index[:, :, None] == jnp.arange(lat_count, dtype=jnp.int32)[None, None, :]).astype(
        jnp.float32
    )
    return jnp.einsum("pio,pia->ao", blocks, onehot, precision=lax.Precision.HIGHEST)


def mix_complex(coefficient, mix_real, mix_imag):
    real_part = coefficient[:, :, 0]
    imag_part = coefficient[:, :, 1]
    out_real = jnp.einsum(
        "lmc,cd->lmd", real_part, mix_real, preferred_element_type=jnp.float32
    ) - jnp.einsum("lmc,cd->lmd", imag_part, mix_imag, preferred_element_type=jnp.float32)
    out_imag = jnp.einsum(
        "lmc,cd->lmd", imag_part, mix_real, preferred_element_type=jnp.float32
    ) + jnp.einsum("lmc,cd->lmd", real_part, mix_imag, preferred_element_type=jnp.float32)
    return jnp.stack([out_real, out_imag], axis=2).astype(jnp.bfloat16)


def spectral_block(spectrum, forward, inverse, mixing):
    lat_count, columns, channels = spectrum.shape
    split = spectrum.reshape(lat_count, columns // 2, 2, channels)
    coefficient = jnp.einsum(
        "mla,amrc->lmrc", forward, split, preferred_element_type=jnp.float32
    ).astype(jnp.bfloat16)
    mixed = mix_complex(coefficient, mixing[0], mixing[1])
    returned = jnp.einsum(
        "mal,lmrc->amrc", inverse, mixed, preferred_element_type=jnp.float32
    ).astype(jnp.bfloat16)
    return returned.reshape(lat_count, columns, channels)


def spectral_adjoint(returned_adjoint, forward, inverse, mixing):
    lat_count, columns, channels = returned_adjoint.shape
    split = returned_adjoint.reshape(lat_count, columns // 2, 2, channels)
    mixed_adjoint = jnp.einsum(
        "mal,amrc->lmrc", inverse, split, preferred_element_type=jnp.float32
    ).astype(jnp.bfloat16)
    real_part = mixed_adjoint[:, :, 0]
    imag_part = mixed_adjoint[:, :, 1]
    back_real = jnp.einsum(
        "lmd,cd->lmc", real_part, mixing[0], preferred_element_type=jnp.float32
    ) + jnp.einsum("lmd,cd->lmc", imag_part, mixing[1], preferred_element_type=jnp.float32)
    back_imag = jnp.einsum(
        "lmd,cd->lmc", imag_part, mixing[0], preferred_element_type=jnp.float32
    ) - jnp.einsum("lmd,cd->lmc", real_part, mixing[1], preferred_element_type=jnp.float32)
    coefficient_adjoint = jnp.stack([back_real, back_imag], axis=2).astype(jnp.bfloat16)
    spectrum_adjoint = jnp.einsum(
        "mla,lmrc->amrc", forward, coefficient_adjoint, preferred_element_type=jnp.float32
    ).astype(jnp.bfloat16)
    return spectrum_adjoint.reshape(lat_count, columns, channels)


def to_modes(values):
    return two_step_exchange(
        values, (("sec", "tile_0", "tile_1", "tile_2"), "tile_3"), (1, 0), 1, 0
    )


def to_bands(values):
    return lax.all_to_all(values, SEC_TILE, split_axis=0, concat_axis=1, tiled=True)


def rims(values, width):
    with_rows = with_halo(values, ((TILE, 0),), width, False)
    return with_halo(with_rows, (("sec", 1),), width, True)


def spread_rows(matrix, values):
    return lax.psum_scatter(
        jnp.dot(matrix, values, precision=lax.Precision.HIGHEST),
        SEC_TILE,
        scatter_dimension=0,
        tiled=True,
    )


def collect_rows(matrix, values, lon_count, fields, offset, half):
    piece = lax.all_gather(values, SEC_TILE, axis=0, tiled=True)
    own = lax.dynamic_slice_in_dim(
        piece.reshape(piece.shape[0], lon_count, fields), offset, half, 1
    )
    return jnp.dot(
        matrix, own.reshape(piece.shape[0], half * fields), precision=lax.Precision.HIGHEST
    )


def place_half(values, lon_count, offset):
    shape = (values.shape[0], lon_count) + values.shape[2:]
    empty = jnp.zeros(shape, jnp.float32)
    starts = (jnp.int32(0), offset) + tuple((jnp.int32(0) for extra in values.shape[2:]))
    return lax.dynamic_update_slice(empty, values, starts)


def per_device(
    atmosphere,
    ocean_state,
    land_mask,
    crossing_bands,
    ocean_regrid,
    atmosphere_regrid,
    surface_read,
    surface_embed,
    flux_read,
    flux_embed,
    legendre_forward,
    legendre_inverse,
    spectral_mix,
    conv_kernel,
    norm_gain,
    expand_weight,
    project_weight,
    atmosphere_cotangent,
    ocean_cotangent,
):
    band_total = lax.axis_size(SEC_TILE)
    lat_rows, lon_count, channels = atmosphere.shape
    lat_count = lat_rows * band_total
    ocean_rows, ocean_lon, ocean_channels = ocean_state.shape
    half = lon_count // lax.axis_size("sec")
    offset = lax.axis_index("sec") * half
    ratio = ocean_lon // half
    flux_count = flux_read.shape[1]
    radius = conv_kernel.shape[1] // 2
    layer_count = conv_kernel.shape[0]
    highest = lax.Precision.HIGHEST
    mask_value = land_mask.astype(jnp.float32)
    to_ocean = ocean_matrix(crossing_bands[0], ocean_regrid[0], lat_count)
    to_atmosphere = atmosphere_matrix(crossing_bands[0], atmosphere_regrid[0], lat_count)
    surface = jnp.dot(ocean_state, surface_read, preferred_element_type=jnp.float32)
    coarse = jnp.mean((mask_value * surface).reshape(ocean_rows, half, ratio), axis=2)
    surface_atmosphere = spread_rows(to_atmosphere, place_half(coarse, lon_count, offset))
    flux = jnp.einsum("agc,cf->agf", atmosphere, flux_read, preferred_element_type=jnp.float32)
    flux_ocean = collect_rows(
        to_ocean,
        flux.reshape(lat_rows, lon_count * flux_count),
        lon_count,
        flux_count,
        offset,
        half,
    )
    mixed_input = (
        atmosphere.astype(jnp.float32)
        + surface_atmosphere[:, :, None] * surface_embed[None, None, :]
    ).astype(jnp.bfloat16)
    table = wave_table(lon_count, legendre_forward.shape[0] * band_total)
    spectrum = jnp.einsum(
        "gk,agc->akc", table, mixed_input, preferred_element_type=jnp.float32
    ).astype(jnp.bfloat16)
    returned = to_bands(
        spectral_block(to_modes(spectrum), legendre_forward, legendre_inverse, spectral_mix)
    )
    response = jnp.einsum("gk,akc->agc", table, returned, preferred_element_type=jnp.float32)
    atmosphere_next = (mixed_input.astype(jnp.float32) + jax.nn.gelu(response)).astype(jnp.bfloat16)
    forcing_coarse = jnp.einsum(
        "ogf,fc->ogc",
        flux_ocean.reshape(ocean_rows, half, flux_count),
        flux_embed.astype(jnp.float32),
        precision=highest,
    )
    forcing = jnp.broadcast_to(
        forcing_coarse[:, :, None, :], (ocean_rows, half, ratio, ocean_channels)
    ).reshape(ocean_rows, ocean_lon, ocean_channels)
    state = (ocean_state.astype(jnp.float32) + mask_value[:, :, None] * forcing).astype(
        jnp.bfloat16
    )
    windows = []
    for layer in range(layer_count):
        window = rims(state, radius)
        windows.append(window)
        update = cell_forward(
            depthwise(window, conv_kernel[layer]),
            norm_gain[layer],
            expand_weight[layer],
            project_weight[layer],
        )
        state = (state.astype(jnp.float32) + mask_value[:, :, None] * update).astype(jnp.bfloat16)
    cotangent = ocean_cotangent.astype(jnp.float32)
    for layer in range(layer_count - 1, -1, -1):
        hidden = depthwise(windows[layer], conv_kernel[layer])
        hidden_adjoint = cell_backward(
            hidden,
            norm_gain[layer],
            expand_weight[layer],
            project_weight[layer],
            mask_value,
            cotangent,
        )
        cotangent = cotangent + depthwise(
            rims(hidden_adjoint, radius), conv_kernel[layer, ::-1, ::-1]
        )
    forcing_adjoint = (
        (mask_value[:, :, None] * cotangent)
        .reshape(ocean_rows, half, ratio, ocean_channels)
        .sum(axis=2)
    )
    flux_ocean_adjoint = jnp.einsum(
        "ogc,fc->ogf", forcing_adjoint, flux_embed.astype(jnp.float32), precision=highest
    )
    full_adjoint = place_half(flux_ocean_adjoint, lon_count, offset)
    flux_adjoint = spread_rows(to_ocean.T, full_adjoint.reshape(ocean_rows, lon_count * flux_count))
    flux_adjoint = flux_adjoint.reshape(lat_rows, lon_count, flux_count)
    from_flux = jnp.einsum(
        "agf,cf->agc", flux_adjoint, flux_read.astype(jnp.float32), precision=highest
    )
    atmosphere_adjoint = atmosphere_cotangent.astype(jnp.float32)
    _, gelu_back = jax.vjp(jax.nn.gelu, response)
    response_adjoint = gelu_back(atmosphere_adjoint)[0].astype(jnp.bfloat16)
    returned_adjoint = jnp.einsum(
        "gk,agc->akc", table, response_adjoint, preferred_element_type=jnp.float32
    ).astype(jnp.bfloat16)
    spectrum_adjoint = to_bands(
        spectral_adjoint(
            to_modes(returned_adjoint), legendre_forward, legendre_inverse, spectral_mix
        )
    )
    input_adjoint = atmosphere_adjoint + jnp.einsum(
        "gk,akc->agc", table, spectrum_adjoint, preferred_element_type=jnp.float32
    )
    atmosphere_grad = input_adjoint + from_flux
    surface_adjoint = jnp.einsum("agc,c->ag", input_adjoint, surface_embed, precision=highest)
    coarse_adjoint = collect_rows(to_atmosphere.T, surface_adjoint, lon_count, 1, offset, half)
    widened_adjoint = jnp.broadcast_to(
        coarse_adjoint[:, :, None], (ocean_rows, half, ratio)
    ).reshape(ocean_rows, ocean_lon)
    surface_grad = mask_value * widened_adjoint / ratio
    ocean_grad = (
        cotangent + surface_grad[:, :, None] * surface_read.astype(jnp.float32)[None, None, :]
    )
    return (atmosphere_next, state, atmosphere_grad, ocean_grad)


def solution(mesh):
    finer = Mesh(
        mesh.devices.reshape(mesh.shape["sec"], 4, 2, 4, 2),
        ("sec", "tile_0", "tile_1", "tile_2", "tile_3"),
    )
    placed = (
        P(SEC_TILE, None, None),
        P(TILE, "sec", None),
        P(TILE, "sec"),
        P(TILE, None),
        P(TILE, None, None, None),
        P(TILE, None, None, None),
        P(),
        P(),
        P(),
        P(),
        P(SEC_TILE, None, None),
        P(SEC_TILE, None, None),
        P(),
        P(),
        P(),
        P(),
        P(),
        P(SEC_TILE, None, None),
        P(TILE, "sec", None),
    )
    return jax.shard_map(
        per_device,
        mesh=finer,
        in_specs=placed,
        out_specs=(
            P(SEC_TILE, None, None),
            P(TILE, "sec", None),
            P(SEC_TILE, None, None),
            P(TILE, "sec", None),
        ),
        check_vma=False,
    )
```

profile of v0, /device:TPU:1, one launch (start us, length us, event | category | flops | bytes accessed | tf_op | source)
XLA Modules:
  0.0 916.0 jit_solution(4656370942096807728)
XLA Ops:
  7.3 2.0 fusion.342
  20.9 140.1 %all-reduce.8.cloned.1.call-done = f32[128,360]{1,0:T(8,128)} async-done(((f32[128,360]{1,0:T(8,128)}), f32[128,360]{1,0:T(8,128)}) %all-reduce.8.cloned.1.call-update) | async-done | bytes 184336
  162.3 4.5 all_to_all.38
  167.6 6.6 all-to-all-start.1
  174.8 8.5 all-to-all-done.1
  183.5 173.7 %all-gather.4.cloned.1.call-done = f32[128,1,2880]{2,1,0:T(1,128)} async-done(((f32[1,1,2880]{2,1,0:T(1,128)}), f32[128,1,2880]{2,1,0:T(1,128)}) %all-gather.4.cloned.1.call-update) | async-done | bytes 1474576 | tf_op jit(solution)/shard_map/all_gather | solution.py:197
  357.2 3.8 copy.78
  364.9 3.4 collective-permute-start
  371.3 3.4 collective-permute-done
  374.7 4.4 collective-permute-done.1
  381.7 13.4 %all-to-all-start.2 = ((bf16[128,2,384]{2,1,0:T(2,128)(2,1)}), bf16[128,2,384]{2,1,0:T(2,128)(2,1)}, u32[]{:S(2)}, u32[]{:S(2)}) async-start(bf16[128,2,384]{2,1,0:T(2,128)(2,1)} %copy.75), calls=%async_computation.2 | async-start | bytes 393216 | tf_op jit(solution)/shard_map/all_to_all | solution.py:179
  395.1 2.0 maximum_convert_fusion
  397.1 20.6 %fusion.376 = (f32[8,720]{1,0:T(8,128)S(1)}, f32[8,720,128]{2,1,0:T(8,128)S(1)}) fusion(f32[128]{0:T(128)S(1)} %get-tuple-element.184, f32[14,726,128]{2,1,0:T(8,128)S(1)} %maximum_convert_fusion, f32[128]{0:T(128)S(1)} %get-tuple-element.185, f32[128]{0:T(128)S(1)} %get-tuple-element.186, f32[128]{0:T(128)S(1)} %get-tuple-element.187, ...), kind=kLoop, calls=%fused_computation.842 | loop fusion | flops 72247680 | bytes 147504128 | tf_op jit(solution)/shard_map/reduce_sum | solution.py:80
  422.0 4.9 add_convert_fusion.1
  428.4 3.5 collective-permute-start.4
  432.0 1.9 collective-permute-start.5
  433.9 2.3 add_convert_fusion.3
  436.2 2.3 fusion.239
  441.2 3.5 all_to_all.39
  445.5 12.4 %all-to-all-start.4 = ((bf16[64,2,1,2,384]{4,3,1,2,0:T(2,128)(2,1)}), bf16[64,2,1,2,384]{4,3,1,2,0:T(2,128)(2,1)}, u32[]{:S(2)}, u32[]{:S(2)}) async-start(bf16[64,2,1,2,384]{4,3,1,2,0:T(2,128)(2,1)} %copy.84), calls=%async_computation.4 | async-start | bytes 393216 | tf_op jit(solution)/shard_map/all_to_all | solution.py:27
  463.2 3.6 all-to-all-done.4
  469.1 3.1 maximum_convert_fusion.1
  472.6 20.5 %fusion.374 = (f32[8,720]{1,0:T(8,128)S(1)}, f32[8,720,128]{2,1,0:T(8,128)S(1)}) fusion(f32[128]{0:T(128)S(1)} %copy-done.101, f32[14,726,128]{2,1,0:T(8,128)S(1)} %maximum_convert_fusion.1, f32[128]{0:T(128)S(1)} %copy-done.102, f32[128]{0:T(128)S(1)} %copy-done.103, f32[128]{0:T(128)S(1)} %copy-done.104, f32[128]{0:T(128)S(1)} %copy-done.105, ...), kind=kLoop, calls=%fused_computation.841 | loop fusion | flops 72247680 | bytes 147504128 | tf_op jit(solution)/shard_map/reduce_sum | solution.py:80
  495.0 5.4 fusion.219
  500.4 15.5 %multiply_reduce_fusion.5 = (f32[8,720]{1,0:T(8,128)S(1)}, f32[8,720]{1,0:T(8,128)S(1)}, f32[8,720,128]{2,1,0:T(8,128)}) fusion(f32[128]{0:T(128)S(1)} %copy-done.44, f32[8,720]{1,0:T(8,128)S(1)} %add_rsqrt_fusion, f32[8,720,128]{2,1,0:T(8,128)} %copy-done.2, f32[8,720]{1,0:T(8,128)S(1)} %broadcast_multiply_fusion.6, ...), kind=kOutput, calls=%fused_computation.438 | convolution fusion | flops 1575555840 | bytes 19551744 | tf_op jit(solution)/shard_map/dot_general | solution.py:98
  515.9 6.9 multiply_convert_fusion.6
  522.9 3.8 collective-permute-start.8
  529.5 3.7 collective-permute-done.8
  533.2 4.4 collective-permute-done.9
  541.3 3.5 maximum_convert_fusion.2
  545.1 64.0 %convert_add_fusion = f32[8,720,128]{2,1,0:T(8,128)} fusion(bf16[8,720,128]{2,1,0:T(8,128)(2,1)S(1)} %copy-done.15, f32[14,726,128]{2,1,0:T(8,128)} %maximum_convert_fusion.2, f32[128]{0:T(128)S(1)} %copy-done.54, f32[128]{0:T(128)S(1)} %copy-done.55, f32[128]{0:T(128)S(1)} %copy-done.56, f32[128]{0:T(128)S(1)} %copy-done.57, f32[128]{0:T(128)S(1)} %copy-done.58, ...), kind=kLoop, calls=%fused_computation.26 | loop fusion | flops 72990720 | bytes 148955648 | tf_op jit(solution)/shard_map/add | solution.py:307
  609.2 13.6 %multiply_reduce_fusion.4 = (f32[8,720]{1,0:T(8,128)S(1)}, f32[8,720]{1,0:T(8,128)S(1)}, f32[8,720,128]{2,1,0:T(8,128)}) fusion(f32[128]{0:T(128)S(1)} %copy-done.43, f32[8,720]{1,0:T(8,128)S(1)} %copy-done.24, f32[8,720,128]{2,1,0:T(8,128)S(1)} %get-tuple-element.17, f32[8,720]{1,0:T(8,128)S(1)} %copy-done.17, bf16[2,128,512]{2,1,0:T(8,128)(2,1)S(1)} %copy-done.20, ...), kind=kOutput, calls=%fused_computation.437 | convolution fusion | flops 1574818560 | bytes 21026304 | tf_op jit(solution)/shard_map/dot_general | solution.py:98
  622.7 7.0 multiply_convert_fusion.4
  632.0 3.0 collective-permute-start.12
  635.0 2.1 collective-permute-start.13
  638.2 13.8 %all-to-all-start.5 = ((bf16[128,2,384]{2,1,0:T(2,128)(2,1)}), bf16[128,2,384]{2,1,0:T(2,128)(2,1)}, u32[]{:S(2)}, u32[]{:S(2)}) async-start(bf16[128,2,384]{2,1,0:T(2,128)(2,1)} %copy.87), calls=%async_computation.5 | async-start | bytes 393216 | tf_op jit(solution)/shard_map/all_to_all | solution.py:179
  653.8 8.3 all-to-all-done.5
  666.9 3.4 maximum_convert_fusion.3
  670.4 59.1 %broadcast_multiply_fusion = (f32[8,720,128]{2,1,0:T(8,128)}, f32[8,720,128]{2,1,0:T(8,128)S(1)}) fusion(f32[8,720]{1,0:T(8,128)S(1)} %copy-done.27, f32[8,720,128]{2,1,0:T(8,128)} %convert_add_fusion, f32[128]{0:T(128)S(1)} %copy-done.47, f32[14,726,128]{2,1,0:T(8,128)} %maximum_convert_fusion.3, f32[128]{0:T(128)S(1)} %copy-done.48, ...), kind=kLoop, calls=%fused_computation.447 | loop fusion | flops 72990720 | bytes 153402368 | tf_op jit(solution)/shard_map/mul | solution.py:311
  729.5 4.5 reduce_sum.115
  734.0 2.5 fusion.332
  737.6 5.0 dynamic_update_slice.7
  742.6 2.4 reshape.455
  745.0 3.4 fusion.390
  748.5 8.4 add_convert_fusion
  756.9 140.1 %all-reduce.10.cloned.1.call-done = (f32[128,2880]{1,0:T(8,128)}, f32[128,360]{1,0:T(8,128)}) async-done(((f32[128,2880]{1,0:T(8,128)}, f32[128,360]{1,0:T(8,128)}), (f32[128,2880]{1,0:T(8,128)}, f32[128,360]{1,0:T(8,128)})) %all-reduce.10.cloned.1.call-update) | async-done | bytes 1658896
  904.0 2.2 fusion.233
  906.2 2.8 multiply_add_fusion
  (394 shorter events, 66.1 us)
Async XLA Ops:
  7.2 373.5 %copy-start = (bf16[1,128,128]{2,1,0:T(8,128)(2,1)S(1)}, bf16[1,128,128]{2,1,0:T(8,128)(2,1)}, u32[]{:S(2)}) copy-start(bf16[1,128,128]{2,1,0:T(8,128)(2,1)} %param.30) | copy-start | bytes 98308
  7.2 153.8 %all-reduce.8.cloned.1.call-start = ((), (), s32[]{:S(2)}) async-start(), calls=%async_computation.7 | async-start | bytes 393216
  9.3 152.4 %copy-start.45 = (f32[384]{0:T(512)S(1)}, f32[384]{0:T(512)}, u32[]{:S(2)}) copy-start(f32[384]{0:T(512)} %param.26) | copy-start | bytes 4612
  13.4 160.8 %copy-start.129 = (f32[2,128]{1,0:T(2,128)S(1)}, f32[2,128]{1,0:T(2,128)}, u32[]{:S(2)}) copy-start(f32[2,128]{1,0:T(2,128)} %param.33) | copy-start | bytes 3076
  13.4 169.9 %copy-start.29 = (bf16[1,128,128]{2,1,0:T(8,128)(2,1)S(1)}, bf16[1,128,128]{2,1,0:T(8,128)(2,1)}, u32[]{:S(2)}) copy-start(bf16[1,128,128]{2,1,0:T(8,128)(2,1)} %param.29) | copy-start | bytes 98308
  13.4 343.8 %all-gather.4.cloned.1.call-start = ((), (), s32[]{:S(2)}) async-start(), calls=%async_computation.6 | async-start | bytes 1519104 | tf_op jit(solution)/shard_map/all_gather | solution.py:197
  14.5 407.5 %copy-start.25 = (f32[8,720]{1,0:T(8,128)}, f32[8,720]{1,0:T(8,128)S(1)}, u32[]{:S(2)}) copy-start(f32[8,720]{1,0:T(8,128)S(1)} %convert_element_type.219) | copy-start | bytes 69124
  16.1 167.4 %copy-start.13 = (bf16[360,128,2]{1,0,2:T(8,128)(2,1)}, bf16[360,128,2]{1,0,2:T(8,128)(2,1)S(1)}, u32[]{:S(2)}) copy-start(bf16[360,128,2]{1,0,2:T(8,128)(2,1)S(1)} %fusion.261) | copy-start | bytes 552964
  16.5 167.0 %copy-start.28 = (bf16[360,256]{0,1:T(8,128)(2,1)}, bf16[360,256]{0,1:T(8,128)(2,1)S(1)}, u32[]{:S(2)}) copy-start(bf16[360,256]{0,1:T(8,128)(2,1)S(1)} %convert_element_type.224) | copy-start | bytes 552964
  16.7 344.4 %copy-start.38 = (f32[128,8]{0,1:T(8,128)}, f32[128,8]{0,1:T(8,128)S(1)}, u32[]{:S(2)}) copy-start(f32[128,8]{0,1:T(8,128)S(1)} %fusion.336) | copy-start | bytes 12292
  19.5 341.5 %copy-start.31 = (f32[7,7,128]{2,1,0:T(8,128)}, f32[7,7,128]{2,1,0:T(8,128)S(1)}, u32[]{:S(2)}) copy-start(f32[7,7,128]{2,1,0:T(8,128)S(1)} %bitcast_convert_fusion) | copy-start | bytes 75268
  167.6 15.6 %all-to-all-start.1 = ((bf16[64,2,1,2,384]{4,3,1,2,0:T(2,128)(2,1)}), bf16[64,2,1,2,384]{4,3,1,2,0:T(2,128)(2,1)S(1)}, u32[]{:S(2)}, u32[]{:S(2)}) async-start(bf16[64,2,1,2,384]{4,3,1,2,0:T(2,128)(2,1)} %copy.72), calls=%async_computation.1 | async-start | bytes 393216 | tf_op jit(solution)/shard_map/all_to_all | solution.py:27
  174.2 188.2 %copy-start.40 = (bf16[8,128]{1,0:T(8,128)(2,1)S(1)}, bf16[8,128]{1,0:T(8,128)(2,1)}, u32[]{:S(2)}) copy-start(bf16[8,128]{1,0:T(8,128)(2,1)} %param.28) | copy-start | bytes 6148
  174.8 244.9 %copy-start.42 = (f32[128]{0:T(128)}, f32[128]{0:T(128)S(1)}, u32[]{:S(2)}) copy-start(f32[128]{0:T(128)S(1)} %get-tuple-element.235) | copy-start | bytes 1540
  364.8 30.3 %copy-start.3 = (bf16[8,720,128]{2,1,0:T(8,128)(2,1)}, bf16[8,720,128]{2,1,0:T(8,128)(2,1)S(1)}, u32[]{:S(2)}) copy-start(bf16[8,720,128]{2,1,0:T(8,128)(2,1)S(1)} %add_convert_fusion.2) | copy-start | bytes 4423684
  364.9 9.8 %collective-permute-start = (bf16[3,720,128]{2,1,0:T(8,128)(2,1)S(1)}, bf16[3,720,128]{2,1,0:T(8,128)(2,1)S(1)}, u32[]{:S(2)}, u32[]{:S(2)}) collective-permute-start(bf16[3,720,128]{2,1,0:T(8,128)(2,1)S(1)} %get-tuple-element.34), channel_id=1, source_target_pairs={{0,1},{1,2},{2,3},{3,4},{4,5},{5,6},{6,7},{7,8},{8,9},{9,10},{10,1... | collective-permute-start | bytes 1658888 | tf_op jit(solution)/shard_map/ppermute | solution.py:44
  368.3 10.8 %collective-permute-start.1 = (bf16[3,720,128]{2,1,0:T(8,128)(2,1)S(1)}, bf16[3,720,128]{2,1,0:T(8,128)(2,1)S(1)}, u32[]{:S(2)}, u32[]{:S(2)}) collective-permute-start(bf16[3,720,128]{2,1,0:T(8,128)(2,1)S(1)} %get-tuple-element.35), channel_id=1, source_target_pairs={{1,0},{2,1},{3,2},{4,3},{5,4},{6,5},{7,6},{8,7},{9,8},{10,9},{11,1... | collective-permute-start | bytes 1658888 | tf_op jit(solution)/shard_map/ppermute | solution.py:45
  379.1 16.0 %collective-permute-start.2 = (bf16[14,3,128]{2,1,0:T(4,128)(2,1)S(1)}, bf16[14,3,128]{2,1,0:T(4,128)(2,1)S(1)}, u32[]{:S(2)}, u32[]{:S(2)}) collective-permute-start(bf16[14,3,128]{2,1,0:T(4,128)(2,1)S(1)} %get-tuple-element.26), channel_id=1, source_target_pairs={{0,64},{64,0},{1,65},{65,1},{2,66},{66,2},{3,67},{67,3},{4,68},{68... | collective-permute-start | bytes 32264 | tf_op jit(solution)/shard_map/ppermute | solution.py:44
  380.4 14.7 %collective-permute-start.3 = (bf16[14,3,128]{2,1,0:T(4,128)(2,1)S(1)}, bf16[14,3,128]{2,1,0:T(4,128)(2,1)S(1)}, u32[]{:S(2)}, u32[]{:S(2)}) collective-permute-start(bf16[14,3,128]{2,1,0:T(4,128)(2,1)S(1)} %get-tuple-element.27), channel_id=1, source_target_pairs={{64,0},{0,64},{65,1},{1,65},{66,2},{2,66},{67,3},{3,67},{68,4},{4,... | collective-permute-start | bytes 32264 | tf_op jit(solution)/shard_map/ppermute | solution.py:45
  381.7 52.2 %all-to-all-start.2 = ((bf16[128,2,384]{2,1,0:T(2,128)(2,1)}), bf16[128,2,384]{2,1,0:T(2,128)(2,1)}, u32[]{:S(2)}, u32[]{:S(2)}) async-start(bf16[128,2,384]{2,1,0:T(2,128)(2,1)} %copy.75), calls=%async_computation.2 | async-start | bytes 393216 | tf_op jit(solution)/shard_map/all_to_all | solution.py:179
  428.4 31.6 %collective-permute-start.4 = (bf16[3,720,128]{2,1,0:T(8,128)(2,1)}, bf16[3,720,128]{2,1,0:T(8,128)(2,1)S(1)}, u32[]{:S(2)}, u32[]{:S(2)}) collective-permute-start(bf16[3,720,128]{2,1,0:T(8,128)(2,1)} %get-tuple-element.32), channel_id=1, source_target_pairs={{0,1},{1,2},{2,3},{3,4},{4,5},{5,6},{6,7},{7,8},{8,9},{9,10},{10,1... | collective-permute-start | bytes 1658888 | tf_op jit(solution)/shard_map/ppermute | solution.py:44
  432.0 28.0 %collective-permute-start.5 = (bf16[3,720,128]{2,1,0:T(8,128)(2,1)}, bf16[3,720,128]{2,1,0:T(8,128)(2,1)}, u32[]{:S(2)}, u32[]{:S(2)}) collective-permute-start(bf16[3,720,128]{2,1,0:T(8,128)(2,1)} %get-tuple-element.33), channel_id=1, source_target_pairs={{1,0},{2,1},{3,2},{4,3},{5,4},{6,5},{7,6},{8,7},{9,8},{10,9},{11,1... | collective-permute-start | bytes 1658888 | tf_op jit(solution)/shard_map/ppermute | solution.py:45
  436.2 23.3 %copy-start.130 = (bf16[128]{0:T(256)(128)(2,1)S(1)}, bf16[128]{0:T(256)(128)(2,1)}, u32[]{:S(2)}) copy-start(bf16[128]{0:T(256)(128)(2,1)} %param.25) | copy-start | bytes 772
  445.5 21.3 %all-to-all-start.4 = ((bf16[64,2,1,2,384]{4,3,1,2,0:T(2,128)(2,1)}), bf16[64,2,1,2,384]{4,3,1,2,0:T(2,128)(2,1)}, u32[]{:S(2)}, u32[]{:S(2)}) async-start(bf16[64,2,1,2,384]{4,3,1,2,0:T(2,128)(2,1)} %copy.84), calls=%async_computation.4 | async-start | bytes 393216 | tf_op jit(solution)/shard_map/all_to_all | solution.py:27
  461.4 7.7 collective-permute-start.6
  462.4 6.6 collective-permute-start.7
  515.9 12.8 %copy-start.10 = (bf16[2,384,384]{2,1,0:T(8,128)(2,1)S(1)}, bf16[2,384,384]{2,1,0:T(8,128)(2,1)}, u32[]{:S(2)}) copy-start(bf16[2,384,384]{2,1,0:T(8,128)(2,1)} %param.31) | copy-start | bytes 1769476
  515.9 12.8 %copy-start.12 = (bf16[128,1,2,384]{0,3,2,1:T(8,128)(2,1)S(1)}, bf16[128,1,2,384]{0,3,2,1:T(8,128)(2,1)}, u32[]{:S(2)}) copy-start(bf16[128,1,2,384]{0,3,2,1:T(8,128)(2,1)} %fusion.236) | copy-start | bytes 589828
  522.9 10.3 %collective-permute-start.8 = (bf16[3,720,128]{2,1,0:T(8,128)(2,1)S(1)}, bf16[3,720,128]{2,1,0:T(8,128)(2,1)S(1)}, u32[]{:S(2)}, u32[]{:S(2)}) collective-permute-start(bf16[3,720,128]{2,1,0:T(8,128)(2,1)S(1)} %get-tuple-element.30), channel_id=1, source_target_pairs={{0,1},{1,2},{2,3},{3,4},{4,5},{5,6},{6,7},{7,8},{8,9},{9,10},{10,1... | collective-permute-start | bytes 1658888 | tf_op jit(solution)/shard_map/ppermute | solution.py:44
  526.8 10.8 %collective-permute-start.9 = (bf16[3,720,128]{2,1,0:T(8,128)(2,1)S(1)}, bf16[3,720,128]{2,1,0:T(8,128)(2,1)S(1)}, u32[]{:S(2)}, u32[]{:S(2)}) collective-permute-start(bf16[3,720,128]{2,1,0:T(8,128)(2,1)S(1)} %get-tuple-element.31), channel_id=1, source_target_pairs={{1,0},{2,1},{3,2},{4,3},{5,4},{6,5},{7,6},{8,7},{9,8},{10,9},{11,1... | collective-permute-start | bytes 1658888 | tf_op jit(solution)/shard_map/ppermute | solution.py:45
  537.6 2.8 collective-permute-start.10
  538.7 2.6 collective-permute-start.11
  545.1 64.1 %copy-start.17 = (f32[8,720]{1,0:T(8,128)S(1)}, f32[8,720]{1,0:T(8,128)}, u32[]{:S(2)}) copy-start(f32[8,720]{1,0:T(8,128)} %copy-done.16) | copy-start | bytes 69124
  545.1 64.1 %copy-start.24 = (f32[8,720]{1,0:T(8,128)S(1)}, f32[8,720]{1,0:T(8,128)}, u32[]{:S(2)}) copy-start(f32[8,720]{1,0:T(8,128)} %copy-done.23) | copy-start | bytes 69124
  545.1 64.1 %copy-start.43 = (f32[128]{0:T(128)S(1)}, f32[128]{0:T(128)}, u32[]{:S(2)}) copy-start(f32[128]{0:T(128)} %copy-done.42) | copy-start | bytes 1540
  622.7 14.4 %copy-start.30 = (bf16[1,128,128]{2,1,0:T(8,128)(2,1)S(1)}, bf16[1,128,128]{2,1,0:T(8,128)(2,1)}, u32[]{:S(2)}) copy-start(bf16[1,128,128]{2,1,0:T(8,128)(2,1)} %param.29) | copy-start | bytes 98308
  630.9 31.2 %copy-start.14 = (bf16[360,128,2]{1,0,2:T(8,128)(2,1)S(1)}, bf16[360,128,2]{1,0,2:T(8,128)(2,1)}, u32[]{:S(2)}) copy-start(bf16[360,128,2]{1,0,2:T(8,128)(2,1)} %copy-done.13) | copy-start | bytes 552964
  632.0 31.5 %copy-start.6 = (bf16[8,720,128]{2,1,0:T(8,128)(2,1)S(1)}, bf16[8,720,128]{2,1,0:T(8,128)(2,1)}, u32[]{:S(2)}) copy-start(bf16[8,720,128]{2,1,0:T(8,128)(2,1)} %copy-done.5) | copy-start | bytes 4423684
  632.0 31.4 %collective-permute-start.12 = (bf16[3,720,128]{2,1,0:T(8,128)(2,1)}, bf16[3,720,128]{2,1,0:T(8,128)(2,1)S(1)}, u32[]{:S(2)}, u32[]{:S(2)}) collective-permute-start(bf16[3,720,128]{2,1,0:T(8,128)(2,1)} %get-tuple-element.28), channel_id=1, source_target_pairs={{0,1},{1,2},{2,3},{3,4},{4,5},{5,6},{6,7},{7,8},{8,9},{9,10},{10,1... | collective-permute-start | bytes 1658888 | tf_op jit(solution)/shard_map/ppermute | solution.py:44
  635.0 28.4 %collective-permute-start.13 = (bf16[3,720,128]{2,1,0:T(8,128)(2,1)}, bf16[3,720,128]{2,1,0:T(8,128)(2,1)S(1)}, u32[]{:S(2)}, u32[]{:S(2)}) collective-permute-start(bf16[3,720,128]{2,1,0:T(8,128)(2,1)} %get-tuple-element.29), channel_id=1, source_target_pairs={{1,0},{2,1},{3,2},{4,3},{5,4},{6,5},{7,6},{8,7},{9,8},{10,9},{11,1... | collective-permute-start | bytes 1658888 | tf_op jit(solution)/shard_map/ppermute | solution.py:45
  638.2 23.8 %all-to-all-start.5 = ((bf16[128,2,384]{2,1,0:T(2,128)(2,1)}), bf16[128,2,384]{2,1,0:T(2,128)(2,1)}, u32[]{:S(2)}, u32[]{:S(2)}) async-start(bf16[128,2,384]{2,1,0:T(2,128)(2,1)} %copy.87), calls=%async_computation.5 | async-start | bytes 393216 | tf_op jit(solution)/shard_map/all_to_all | solution.py:179
  652.1 244.9 %all-reduce.10.cloned.1.call-start = ((), (), s32[]{:S(2)}) async-start(), calls=%async_computation.8 | async-start | bytes 3407872
  663.5 3.4 collective-permute-start.14
  664.1 2.8 collective-permute-start.15
  748.4 148.6 %copy-start.37 = (f32[128,8]{0,1:T(8,128)S(1)}, f32[128,8]{0,1:T(8,128)}, u32[]{:S(2)}) copy-start(f32[128,8]{0,1:T(8,128)} %copy-done.36) | copy-start | bytes 12292
  748.4 152.5 %copy-start.22 = (s32[8,720]{1,0:T(8,128)S(1)}, s32[8,720]{1,0:T(8,128)}, u32[]{:S(2)}) copy-start(s32[8,720]{1,0:T(8,128)} %param.21) | copy-start | bytes 69124
  748.5 155.6 %copy-start.35 = (bf16[384,8]{0,1:T(8,128)(2,1)S(1)}, bf16[384,8]{0,1:T(8,128)(2,1)}, u32[]{:S(2)}) copy-start(bf16[384,8]{0,1:T(8,128)(2,1)} %param.27) | copy-start | bytes 18436
  748.5 157.7 %copy-start.131 = (f32[128]{0:T(128)S(1)}, f32[128]{0:T(128)}, u32[]{:S(2)}) copy-start(f32[128]{0:T(128)} %convert_element_type.275) | copy-start | bytes 1540
  (110 other events, 462.6 us)
Sparse Core Ops, SparseCore 0:
  13.5 147.4 all-reduce.7
  163.3 193.8 all-gather.3
  748.6 148.3 all-reduce.9
where the time goes:
time: 925 us; the launch traced here: 916 us
  waiting for transfers between devices  492 us (53%)
  other arithmetic  207 us (22%)
  matrix products  76.9 us (8%)
  starting transfers between devices  74.6 us (8%)
  local copies, waits for them, and re-layouts  41 us (4%)
  between operations  16.7 us (2%)
    unnamed x5, waiting for transfers between devices  280 us
    all_gather x1, waiting for transfers between devices, collect_rows(): piece = lax.all_gather(values, SEC_TILE, axis=0, tiled=True)  174 us
    add x1, other arithmetic, per_device(): cotangent + depthwise(rims(hidden_adjoint, radius), conv_kernel[layer, ::...  64 us
    mul x1, other arithmetic, per_device(): mask_value[:, :, None] * cotangent  59.1 us
    reduce_sum x2, other arithmetic, cell_forward(): center = hidden - jnp.mean(hidden, axis=-1, keepdims=True)  41.2 us
    dot_general x2, matrix products, cell_backward(): jnp.dot(before_adjoint, expand.T, preferred_element_type=jnp.float32)  29 us
    all_to_all x2, starting transfers between devices, to_bands(): lax.all_to_all(values, SEC_TILE, split_axis=0, concat_axis=1, tiled=True)  27.2 us
    all_to_all x2, starting transfers between devices, turned_blocks(): lax.all_to_all(blocks, axes[k], split_axis=k, concat_axis=k, tiled=True)  19 us
  transfers between devices with their start and end apart: 23, of which 12 were waited for; matrix products, arithmetic and copies ran while one was open for 8% of the time, Pallas kernels for 0%

commit v1 on v0

--- a/solution.py
+++ b/solution.py
@@ -194,7 +194,10 @@
 
 
 def collect_rows(matrix, values, lon_count, fields, offset, half):
-    piece = lax.all_gather(values, SEC_TILE, axis=0, tiled=True)
+    count = lax.axis_size(SEC_TILE)
+    pieces = jnp.stack([values for _ in range(count)])
+    pieces = lax.all_to_all(pieces, SEC_TILE, split_axis=0, concat_axis=0)
+    piece = jnp.concatenate(pieces, axis=0)
     own = lax.dynamic_slice_in_dim(
         piece.reshape(piece.shape[0], lon_count, fields), offset, half, 1
     )

time: 925 us -> 680 us (0.74)
  waiting for transfers between devices: 492 us -> 235 us
  blocking collectives: 8.01 us -> 40.2 us
  starting transfers between devices: 74.6 us -> 59.4 us
    all_gather x1 -> x0, waiting for transfers between devices: 174 us -> none  [collect_rows(): piece = lax.all_gather(values, SEC_TILE, axis=0, tiled=True)]
    unnamed x5 -> x2, waiting for transfers between devices: 280 us -> 162 us
    all_to_all x0 -> x2, waiting for transfers between devices: none -> 30.6 us  [collect_rows(): pieces = lax.all_to_all(pieces, SEC_TILE, split_axis=0, concat_axis=0)]
    all_to_all x0 -> x2, starting transfers between devices: none -> 21.4 us  [collect_rows(): pieces = lax.all_to_all(pieces, SEC_TILE, split_axis=0, concat_axis=0)]
    all_to_all x2 -> x1, starting transfers between devices: 27.2 us -> 6.18 us  [to_bands(): lax.all_to_all(values, SEC_TILE, split_axis=0, concat_axis=1, tiled=True)]
    all_to_all x2 -> x3, blocking collectives: 8.01 us -> 24.7 us  [turned_blocks(): lax.all_to_all(blocks, axes[k], split_axis=k, concat_axis=k, tiled=True)]
    all_to_all x0 -> x1, blocking collectives: none -> 15.5 us  [to_bands(): lax.all_to_all(values, SEC_TILE, split_axis=0, concat_axis=1, tiled=True)]
    all_to_all x2 -> x1, starting transfers between devices: 19 us -> 4.74 us  [turned_blocks(): lax.all_to_all(blocks, axes[k], split_axis=k, concat_axis=k, tiled=True)]
  transfers between devices with their start and end apart: 23 -> 21, of which waited for: 12 -> 19; matrix products, arithmetic and copies ran while one was open for 8% -> 5% of each run, Pallas kernels for 0% -> 0%
where the time goes in v1:
time: 680 us; the launch traced here: 673 us
  waiting for transfers between devices  235 us (35%)
  other arithmetic  205 us (30%)
  matrix products  79.2 us (12%)
  starting transfers between devices  59.4 us (9%)
  blocking collectives  40.2 us (6%)
  local copies, waits for them, and re-layouts  38.4 us (6%)
  between operations  16.4 us (2%)
    unnamed x2, waiting for transfers between devices  162 us
    mul x1, other arithmetic, per_device(): mask_value[:, :, None] * cotangent  59.5 us
    add x1, other arithmetic, per_device(): cotangent + depthwise(rims(hidden_adjoint, radius), conv_kernel[layer, ::...  59.3 us
    reduce_sum x2, other arithmetic, cell_forward(): center = hidden - jnp.mean(hidden, axis=-1, keepdims=True)  41.2 us
    all_to_all x2, waiting for transfers between devices, collect_rows(): pieces = lax.all_to_all(pieces, SEC_TILE, split_axis=0, concat_axis=0)  30.6 us
    dot_general x2, matrix products, cell_backward(): jnp.dot(before_adjoint, expand.T, preferred_element_type=jnp.float32)  29.1 us
    all_to_all x3, blocking collectives, turned_blocks(): lax.all_to_all(blocks, axes[k], split_axis=k, concat_axis=k, tiled=True)  24.7 us
    ppermute x8, waiting for transfers between devices, with_halo(): after = lax.ppermute(first, axis, down)  21.7 us
  transfers between devices with their start and end apart: 21, of which 19 were waited for; matrix products, arithmetic and copies ran while one was open for 5% of the time, Pallas kernels for 0%

profile of v1, /device:TPU:1, one launch (start us, length us, event | category | flops | bytes accessed | tf_op | source)
XLA Modules:
  0.0 673.2 jit_solution(7410057872277585765)
XLA Ops:
  10.5 11.5 %all-to-all-start.3 = ((f32[128,1,2880]{2,1,0:T(1,128)}), f32[128,1,2880]{2,1,0:T(1,128)S(1)}, u32[]{:S(2)}, u32[]{:S(2)}) async-start(f32[128,1,2880]{2,1,0:T(1,128)} %stack.22), calls=%async_computation.3 | async-start | bytes 3014656 | tf_op jit(solution)/shard_map/all_to_all | solution.py:199
  23.1 22.7 %all-to-all-done.3 = f32[128,1,2880]{2,1,0:T(1,128)S(1)} async-done(((f32[128,1,2880]{2,1,0:T(1,128)}), f32[128,1,2880]{2,1,0:T(1,128)S(1)}, u32[]{:S(2)}, u32[]{:S(2)}) %all-to-all-start.3) | async-done | bytes 1474592 | tf_op jit(solution)/shard_map/all_to_all | solution.py:199
  52.4 3.4 collective-permute-start
  59.1 3.5 collective-permute-done
  62.6 4.1 collective-permute-done.1
  69.9 1.9 maximum_convert_fusion
  72.1 20.6 %fusion.375 = (f32[8,720]{1,0:T(8,128)S(1)}, f32[8,720,128]{2,1,0:T(8,128)S(1)}) fusion(f32[128]{0:T(128)S(1)} %copy-done.69, f32[14,726,128]{2,1,0:T(8,128)S(1)} %maximum_convert_fusion, f32[128]{0:T(128)S(1)} %copy-done.70, f32[128]{0:T(128)S(1)} %copy-done.71, f32[128]{0:T(128)S(1)} %copy-done.72, f32[128]{0:T(128)S(1)} %copy-done.73, ...), kind=kLoop, calls=%fused_computation.842 | loop fusion | flops 72247680 | bytes 147504128 | tf_op jit(solution)/shard_map/reduce_sum | solution.py:80
  96.5 4.9 add_convert_fusion.1
  101.5 2.9 collective-permute-start.4
  108.3 2.6 collective-permute-done.4
  110.8 4.7 collective-permute-done.5
  119.7 1.9 maximum_convert_fusion.1
  121.6 20.6 %fusion.373 = (f32[8,720]{1,0:T(8,128)S(1)}, f32[8,720,128]{2,1,0:T(8,128)S(1)}) fusion(f32[128]{0:T(128)S(1)} %get-tuple-element.135, f32[14,726,128]{2,1,0:T(8,128)S(1)} %maximum_convert_fusion.1, f32[128]{0:T(128)S(1)} %get-tuple-element.136, f32[128]{0:T(128)S(1)} %get-tuple-element.137, f32[128]{0:T(128)S(1)} %get-tuple-element.138, ...), kind=kLoop, calls=%fused_computation.841 | loop fusion | flops 72247680 | bytes 147504128 | tf_op jit(solution)/shard_map/reduce_sum | solution.py:80
  144.1 5.4 fusion.219
  149.5 15.5 %multiply_reduce_fusion.5 = (f32[8,720]{1,0:T(8,128)S(1)}, f32[8,720]{1,0:T(8,128)S(1)}, f32[8,720,128]{2,1,0:T(8,128)}) fusion(f32[128]{0:T(128)S(1)} %get-tuple-element.234, f32[8,720]{1,0:T(8,128)S(1)} %add_rsqrt_fusion, f32[8,720,128]{2,1,0:T(8,128)} %copy-done.1, f32[8,720]{1,0:T(8,128)S(1)} %broadcast_multiply_fusion.6, ...), kind=kOutput, calls=%fused_computation.438 | convolution fusion | flops 1575555840 | bytes 19551744 | tf_op jit(solution)/shard_map/dot_general | solution.py:98
  165.0 6.8 %multiply_convert_fusion.6 = bf16[8,720,128]{2,1,0:T(8,128)(2,1)S(1)} fusion(f32[8,720,128]{2,1,0:T(8,128)} %get-tuple-element.236, f32[8,720,128]{2,1,0:T(8,128)} %copy-done.1, f32[8,720]{1,0:T(8,128)S(1)} %broadcast_multiply_fusion.4, f32[8,720]{1,0:T(8,128)S(1)} %broadcast_multiply_fusion.5, f32[128]{0:T(128)S(1)} %get-tuple-element.234, ...), kind=kLoop, calls=%fused_computation.422 | loop fusion | flops 5898240 | bytes 7465472 | tf_op jit(solution)/shard_map/convert_element_type | solution.py:105
  174.1 3.2 collective-permute-start.8
  177.3 1.9 collective-permute-start.9
  194.7 4.3 maximum_convert_fusion.2
  199.2 59.3 %convert_add_fusion = f32[8,720,128]{2,1,0:T(8,128)} fusion(bf16[8,720,128]{2,1,0:T(8,128)(2,1)S(1)} %copy-done.14, f32[14,726,128]{2,1,0:T(8,128)} %maximum_convert_fusion.2, f32[128]{0:T(128)} %get-tuple-element.86, f32[128]{0:T(128)} %get-tuple-element.87, f32[128]{0:T(128)} %get-tuple-element.88, f32[128]{0:T(128)} %get-tuple-element.89, ...), kind=kLoop, calls=%fused_computation.26 | loop fusion | flops 72990720 | bytes 148955648 | tf_op jit(solution)/shard_map/add | solution.py:310
  258.6 13.6 %multiply_reduce_fusion.4 = (f32[8,720]{1,0:T(8,128)S(1)}, f32[8,720]{1,0:T(8,128)S(1)}, f32[8,720,128]{2,1,0:T(8,128)}) fusion(f32[128]{0:T(128)S(1)} %get-tuple-element.235, f32[8,720]{1,0:T(8,128)S(1)} %copy-done.22, f32[8,720,128]{2,1,0:T(8,128)S(1)} %get-tuple-element.17, f32[8,720]{1,0:T(8,128)S(1)} %copy-done.16, ...), kind=kOutput, calls=%fused_computation.437 | convolution fusion | flops 1574818560 | bytes 21026304 | tf_op jit(solution)/shard_map/dot_general | solution.py:98
  272.2 7.1 %multiply_convert_fusion.4 = bf16[8,720,128]{2,1,0:T(8,128)(2,1)S(1)} fusion(f32[8,720,128]{2,1,0:T(8,128)} %get-tuple-element.237, f32[8,720,128]{2,1,0:T(8,128)S(1)} %get-tuple-element.17, f32[8,720]{1,0:T(8,128)S(1)} %broadcast_multiply_fusion.2, f32[8,720]{1,0:T(8,128)S(1)} %broadcast_multiply_fusion.3, f32[128]{0:T(128)S(1)} %get-tuple-element.235, ...), kind=kLoop, calls=%fused_computation.419 | loop fusion | flops 5898240 | bytes 7465472 | tf_op jit(solution)/shard_map/convert_element_type | solution.py:105
  281.3 2.0 collective-permute-start.12
  283.3 2.4 collective-permute-start.13
  287.9 2.1 collective-permute-done.12
  290.0 4.1 collective-permute-done.13
  297.7 6.3 collective-permute-done.15
  304.0 3.4 maximum_convert_fusion.3
  307.5 59.5 %broadcast_multiply_fusion = (f32[8,720,128]{2,1,0:T(8,128)}, f32[8,720,128]{2,1,0:T(8,128)S(1)}) fusion(f32[8,720]{1,0:T(8,128)S(1)} %copy-done.24, f32[8,720,128]{2,1,0:T(8,128)} %convert_add_fusion, f32[128]{0:T(128)S(1)} %get-tuple-element.37, f32[14,726,128]{2,1,0:T(8,128)} %maximum_convert_fusion.3, f32[128]{0:T(128)S(1)} %get-tuple-element.38, ...), kind=kLoop, calls=%fused_computation.447 | loop fusion | flops 72990720 | bytes 153402368 | tf_op jit(solution)/shard_map/mul | solution.py:314
  367.1 4.5 reduce_sum.115
  371.5 2.4 fusion.332
  375.2 5.0 dynamic_update_slice.7
  382.0 2.5 fusion.389
  386.4 161.7 %all-reduce.5.cloned.1.call-done = (f32[128,360]{1,0:T(8,128)}, f32[128,2880]{1,0:T(8,128)}) async-done(((f32[128,360]{1,0:T(8,128)}, f32[128,2880]{1,0:T(8,128)}), (f32[128,360]{1,0:T(8,128)}, f32[128,2880]{1,0:T(8,128)})) %all-reduce.5.cloned.1.call-update) | async-done | bytes 1658896
  548.8 2.1 fusion.238
  552.0 4.2 all_to_all.48
  556.4 16.1 %all_to_all.49 = bf16[64,2,1,2,384]{4,3,1,2,0:T(2,128)(2,1)S(1)} all-to-all(bf16[64,2,1,2,384]{4,3,1,2,0:T(2,128)(2,1)S(1)} %copy.72), channel_id=1, replica_groups=mesh['sec'=2,'tile_0'=4,'tile_1'=2,'tile_2'=4,'tile_3'=2] {'sec','tile_0..., dimensions={0} | all-to-all | bytes 393216 | tf_op jit(solution)/shard_map/all_to_all | solution.py:27
  577.8 15.5 %all_to_all.50 = bf16[128,2,384]{2,1,0:T(2,128)(2,1)S(1)} all-to-all(bf16[128,2,384]{2,1,0:T(2,128)(2,1)S(1)} %copy.75), channel_id=1, replica_groups=mesh['sec'=2,'tile_0'=4,'tile_1'=2,'tile_2'=4,'tile_3'=2] {'sec','tile_0..., dimensions={0} | all-to-all | bytes 393216 | tf_op jit(solution)/shard_map/all_to_all | solution.py:179
  593.3 2.1 add_convert_fusion.3
  597.2 4.3 all_to_all.51
  602.3 4.7 all-to-all-start.5
  607.1 9.0 %all-to-all-done.5 = bf16[64,2,1,2,384]{4,3,1,2,0:T(2,128)(2,1)S(1)} async-done(((bf16[64,2,1,2,384]{4,3,1,2,0:T(2,128)(2,1)}), bf16[64,2,1,2,384]{4,3,1,2,0:T(2,128)(2,1)S(1)}, u32[]{:S(2)}, u32[]{:S(2)}) %all-to-all-start.5) | async-done | bytes 196640 | tf_op jit(solution)/shard_map/all_to_all | solution.py:27
  622.3 6.2 all-to-all-start.6
  628.5 8.1 %add_convert_fusion = bf16[8,720,128]{2,1,0:T(8,128)(2,1)} fusion(bf16[8,720,128]{2,1,0:T(8,128)(2,1)} %copy-done.9, f32[8,720,512]{2,1,0:T(8,128)} %fusion.219, f32[8,720]{1,0:T(8,128)S(1)} %copy-done.24, bf16[2,512,128]{2,1,0:T(8,128)(2,1)} %param.35), kind=kOutput, calls=%fused_computation.424 | convolution fusion | flops 784465920 | bytes 14899712 | tf_op jit(solution)/shard_map/dot_general | solution.py:85
  641.5 9.9 %all-to-all-start.7 = ((f32[128,1,360]{2,1,0:T(1,128)}), f32[128,1,360]{2,1,0:T(1,128)}, u32[]{:S(2)}, u32[]{:S(2)}) async-start(f32[128,1,360]{2,1,0:T(1,128)} %stack.26), calls=%async_computation.7 | async-start | bytes 393216 | tf_op jit(solution)/shard_map/all_to_all | solution.py:199
  651.5 2.2 fusion.233
  653.6 7.9 %all-to-all-done.7 = f32[128,1,360]{2,1,0:T(1,128)} async-done(((f32[128,1,360]{2,1,0:T(1,128)}), f32[128,1,360]{2,1,0:T(1,128)}, u32[]{:S(2)}, u32[]{:S(2)}) %all-to-all-start.7) | async-done | bytes 184352 | tf_op jit(solution)/shard_map/all_to_all | solution.py:199
  664.1 2.0 multiply_add_fusion
  (339 shorter events, 84.2 us)
Async XLA Ops:
  7.2 568.6 %copy-start = (bf16[1,128,128]{2,1,0:T(8,128)(2,1)S(1)}, bf16[1,128,128]{2,1,0:T(8,128)(2,1)}, u32[]{:S(2)}) copy-start(bf16[1,128,128]{2,1,0:T(8,128)(2,1)} %param.30) | copy-start | bytes 98308
  7.2 14.8 %copy-start.20 = (s32[8,720]{1,0:T(8,128)S(1)}, s32[8,720]{1,0:T(8,128)}, u32[]{:S(2)}) copy-start(s32[8,720]{1,0:T(8,128)} %param.21) | copy-start | bytes 69124
  7.2 14.9 %copy-start.105 = (f32[1,4,8,1]{2,3,1,0:T(1,128)S(1)}, f32[1,4,8,1]{2,3,1,0:T(1,128)}, u32[]{:S(2)}) copy-start(f32[1,4,8,1]{2,3,1,0:T(1,128)} %param.23) | copy-start | bytes 388
  7.2 14.9 %copy-start.107 = (s32[1,4]{1,0:T(1,128)S(1)}, s32[1,4]{1,0:T(1,128)}, u32[]{:S(2)}) copy-start(s32[1,4]{1,0:T(1,128)} %param.22) | copy-start | bytes 52
  7.2 15.0 %copy-start.28 = (bf16[2,7,7,128]{3,0,2,1:T(2,128)(2,1)S(1)}, bf16[2,7,7,128]{3,0,2,1:T(2,128)(2,1)}, u32[]{:S(2)}) copy-start(bf16[2,7,7,128]{3,0,2,1:T(2,128)(2,1)} %param.32) | copy-start | bytes 75268
  10.5 35.3 %all-to-all-start.3 = ((f32[128,1,2880]{2,1,0:T(1,128)}), f32[128,1,2880]{2,1,0:T(1,128)S(1)}, u32[]{:S(2)}, u32[]{:S(2)}) async-start(f32[128,1,2880]{2,1,0:T(1,128)} %stack.22), calls=%async_computation.3 | async-start | bytes 3014656 | tf_op jit(solution)/shard_map/all_to_all | solution.py:199
  22.0 27.1 %copy-start.32 = (bf16[8,128]{1,0:T(8,128)(2,1)S(1)}, bf16[8,128]{1,0:T(8,128)(2,1)}, u32[]{:S(2)}) copy-start(bf16[8,128]{1,0:T(8,128)(2,1)} %param.28) | copy-start | bytes 6148
  22.0 526.1 %all-reduce.5.cloned.1.call-start = ((), (), s32[]{:S(2)}) async-start(), calls=%async_computation.8 | async-start | bytes 3407872
  22.0 127.5 %copy-start.23 = (f32[8,720]{1,0:T(8,128)}, f32[8,720]{1,0:T(8,128)S(1)}, u32[]{:S(2)}) copy-start(f32[8,720]{1,0:T(8,128)S(1)} %convert_element_type.219) | copy-start | bytes 69124
  22.3 27.7 %copy-start.30 = (f32[128,8]{0,1:T(8,128)}, f32[128,8]{0,1:T(8,128)S(1)}, u32[]{:S(2)}) copy-start(f32[128,8]{0,1:T(8,128)S(1)} %fusion.336) | copy-start | bytes 12292
  51.5 20.4 %copy-start.2 = (bf16[8,720,128]{2,1,0:T(8,128)(2,1)}, bf16[8,720,128]{2,1,0:T(8,128)(2,1)S(1)}, u32[]{:S(2)}) copy-start(bf16[8,720,128]{2,1,0:T(8,128)(2,1)S(1)} %add_convert_fusion.2) | copy-start | bytes 4423684
  52.4 10.2 %collective-permute-start = (bf16[3,720,128]{2,1,0:T(8,128)(2,1)}, bf16[3,720,128]{2,1,0:T(8,128)(2,1)S(1)}, u32[]{:S(2)}, u32[]{:S(2)}) collective-permute-start(bf16[3,720,128]{2,1,0:T(8,128)(2,1)} %get-tuple-element.34), channel_id=1, source_target_pairs={{0,1},{1,2},{2,3},{3,4},{4,5},{5,6},{6,7},{7,8},{8,9},{9,10},{10,1... | collective-permute-start | bytes 1658888 | tf_op jit(solution)/shard_map/ppermute | solution.py:44
  55.9 10.8 %collective-permute-start.1 = (bf16[3,720,128]{2,1,0:T(8,128)(2,1)S(1)}, bf16[3,720,128]{2,1,0:T(8,128)(2,1)S(1)}, u32[]{:S(2)}, u32[]{:S(2)}) collective-permute-start(bf16[3,720,128]{2,1,0:T(8,128)(2,1)S(1)} %get-tuple-element.35), channel_id=1, source_target_pairs={{1,0},{2,1},{3,2},{4,3},{5,4},{6,5},{7,6},{8,7},{9,8},{10,9},{11,1... | collective-permute-start | bytes 1658888 | tf_op jit(solution)/shard_map/ppermute | solution.py:45
  58.5 47.8 %copy-start.27 = (f32[7,7,128]{2,1,0:T(8,128)}, f32[7,7,128]{2,1,0:T(8,128)S(1)}, u32[]{:S(2)}) copy-start(f32[7,7,128]{2,1,0:T(8,128)S(1)} %bitcast_convert_fusion.1) | copy-start | bytes 75268
  66.7 3.0 collective-permute-start.2
  66.8 3.1 collective-permute-start.3
  101.4 18.3 %copy-start.9 = (bf16[8,720,128]{2,1,0:T(8,128)(2,1)}, bf16[8,720,128]{2,1,0:T(8,128)(2,1)S(1)}, u32[]{:S(2)}) copy-start(bf16[8,720,128]{2,1,0:T(8,128)(2,1)S(1)} %add_convert_fusion.1) | copy-start | bytes 4423684
  101.5 9.3 %collective-permute-start.4 = (bf16[3,720,128]{2,1,0:T(8,128)(2,1)S(1)}, bf16[3,720,128]{2,1,0:T(8,128)(2,1)S(1)}, u32[]{:S(2)}, u32[]{:S(2)}) collective-permute-start(bf16[3,720,128]{2,1,0:T(8,128)(2,1)S(1)} %get-tuple-element.32), channel_id=1, source_target_pairs={{0,1},{1,2},{2,3},{3,4},{4,5},{5,6},{6,7},{7,8},{8,9},{9,10},{10,1... | collective-permute-start | bytes 1658888 | tf_op jit(solution)/shard_map/ppermute | solution.py:44
  104.4 11.1 %collective-permute-start.5 = (bf16[3,720,128]{2,1,0:T(8,128)(2,1)S(1)}, bf16[3,720,128]{2,1,0:T(8,128)(2,1)S(1)}, u32[]{:S(2)}, u32[]{:S(2)}) collective-permute-start(bf16[3,720,128]{2,1,0:T(8,128)(2,1)S(1)} %get-tuple-element.33), channel_id=1, source_target_pairs={{1,0},{2,1},{3,2},{4,3},{5,4},{6,5},{7,6},{8,7},{9,8},{10,9},{11,1... | collective-permute-start | bytes 1658888 | tf_op jit(solution)/shard_map/ppermute | solution.py:45
  115.5 2.7 collective-permute-start.6
  116.9 2.7 collective-permute-start.7
  174.1 13.5 %collective-permute-start.8 = (bf16[3,720,128]{2,1,0:T(8,128)(2,1)}, bf16[3,720,128]{2,1,0:T(8,128)(2,1)S(1)}, u32[]{:S(2)}, u32[]{:S(2)}) collective-permute-start(bf16[3,720,128]{2,1,0:T(8,128)(2,1)} %get-tuple-element.30), channel_id=1, source_target_pairs={{0,1},{1,2},{2,3},{3,4},{4,5},{5,6},{6,7},{7,8},{8,9},{9,10},{10,1... | collective-permute-start | bytes 1658888 | tf_op jit(solution)/shard_map/ppermute | solution.py:44
  177.3 11.1 %collective-permute-start.9 = (bf16[3,720,128]{2,1,0:T(8,128)(2,1)}, bf16[3,720,128]{2,1,0:T(8,128)(2,1)}, u32[]{:S(2)}, u32[]{:S(2)}) collective-permute-start(bf16[3,720,128]{2,1,0:T(8,128)(2,1)} %get-tuple-element.31), channel_id=1, source_target_pairs={{1,0},{2,1},{3,2},{4,3},{5,4},{6,5},{7,6},{8,7},{9,8},{10,9},{11,1... | collective-permute-start | bytes 1658888 | tf_op jit(solution)/shard_map/ppermute | solution.py:45
  189.2 5.4 collective-permute-start.10
  189.3 5.4 collective-permute-start.11
  199.2 59.4 %copy-start.16 = (f32[8,720]{1,0:T(8,128)S(1)}, f32[8,720]{1,0:T(8,128)}, u32[]{:S(2)}) copy-start(f32[8,720]{1,0:T(8,128)} %copy-done.15) | copy-start | bytes 69124
  199.2 59.4 %copy-start.19 = (bf16[2,128,512]{2,1,0:T(8,128)(2,1)S(1)}, bf16[2,128,512]{2,1,0:T(8,128)(2,1)}, u32[]{:S(2)}) copy-start(bf16[2,128,512]{2,1,0:T(8,128)(2,1)} %param.34) | copy-start | bytes 786436
  199.2 59.4 %copy-start.22 = (f32[8,720]{1,0:T(8,128)S(1)}, f32[8,720]{1,0:T(8,128)}, u32[]{:S(2)}) copy-start(f32[8,720]{1,0:T(8,128)} %copy-done.21) | copy-start | bytes 69124
  199.2 59.4 %copy-start.24 = (f32[8,720]{1,0:T(8,128)S(1)}, f32[8,720]{1,0:T(8,128)}, u32[]{:S(2)}) copy-start(f32[8,720]{1,0:T(8,128)} %copy-done.23) | copy-start | bytes 69124
  272.2 13.6 %copy-start.106 = (f32[1,4,1,8]{3,2,1,0:T(1,128)S(1)}, f32[1,4,1,8]{3,2,1,0:T(1,128)}, u32[]{:S(2)}) copy-start(f32[1,4,1,8]{3,2,1,0:T(1,128)} %param.24) | copy-start | bytes 388
  272.2 13.6 %copy-start.108 = (s32[1,4]{1,0:T(1,128)S(1)}, s32[1,4]{1,0:T(1,128)}, u32[]{:S(2)}) copy-start(s32[1,4]{1,0:T(1,128)} %param.22) | copy-start | bytes 52
  272.2 13.8 %copy-start.17 = (f32[8,180]{0,1:T(8,128)S(1)}, f32[8,180]{0,1:T(8,128)}, u32[]{:S(2)}) copy-start(f32[8,180]{0,1:T(8,128)} %broadcast_multiply_fusion.1) | copy-start | bytes 17284
  272.2 14.6 %copy-start.26 = (f32[7,7,128]{2,1,0:T(8,128)S(1)}, f32[7,7,128]{2,1,0:T(8,128)}, u32[]{:S(2)}) copy-start(f32[7,7,128]{2,1,0:T(8,128)} %bitcast_convert_fusion) | copy-start | bytes 75268
  281.3 22.7 %copy-start.7 = (bf16[8,720,128]{2,1,0:T(8,128)(2,1)S(1)}, bf16[8,720,128]{2,1,0:T(8,128)(2,1)}, u32[]{:S(2)}) copy-start(bf16[8,720,128]{2,1,0:T(8,128)(2,1)} %copy-done.6) | copy-start | bytes 4423684
  281.3 8.8 %collective-permute-start.12 = (bf16[3,720,128]{2,1,0:T(8,128)(2,1)}, bf16[3,720,128]{2,1,0:T(8,128)(2,1)S(1)}, u32[]{:S(2)}, u32[]{:S(2)}) collective-permute-start(bf16[3,720,128]{2,1,0:T(8,128)(2,1)} %get-tuple-element.28), channel_id=1, source_target_pairs={{0,1},{1,2},{2,3},{3,4},{4,5},{5,6},{6,7},{7,8},{8,9},{9,10},{10,1... | collective-permute-start | bytes 1658888 | tf_op jit(solution)/shard_map/ppermute | solution.py:44
  283.3 10.8 %collective-permute-start.13 = (bf16[3,720,128]{2,1,0:T(8,128)(2,1)S(1)}, bf16[3,720,128]{2,1,0:T(8,128)(2,1)S(1)}, u32[]{:S(2)}, u32[]{:S(2)}) collective-permute-start(bf16[3,720,128]{2,1,0:T(8,128)(2,1)S(1)} %get-tuple-element.29), channel_id=1, source_target_pairs={{1,0},{2,1},{3,2},{4,3},{5,4},{6,5},{7,6},{8,7},{9,8},{10,9},{11,1... | collective-permute-start | bytes 1658888 | tf_op jit(solution)/shard_map/ppermute | solution.py:45
  294.9 2.8 collective-permute-start.14
  296.4 7.5 %collective-permute-start.15 = (bf16[14,3,128]{2,1,0:T(4,128)(2,1)S(1)}, bf16[14,3,128]{2,1,0:T(4,128)(2,1)S(1)}, u32[]{:S(2)}, u32[]{:S(2)}) collective-permute-start(bf16[14,3,128]{2,1,0:T(4,128)(2,1)S(1)} %get-tuple-element.21), channel_id=1, source_target_pairs={{64,0},{0,64},{65,1},{1,65},{66,2},{2,66},{67,3},{3,67},{68,4},{4,... | collective-permute-start | bytes 32264 | tf_op jit(solution)/shard_map/ppermute | solution.py:45
  296.6 10.8 %copy-start.50 = (f32[128]{0:T(128)S(1)}, f32[128]{0:T(128)}, u32[]{:S(2)}) copy-start(f32[128]{0:T(128)} %get-tuple-element.55) | copy-start | bytes 1540
  380.1 168.7 %copy-start.34 = (f32[384]{0:T(512)S(1)}, f32[384]{0:T(512)}, u32[]{:S(2)}) copy-start(f32[384]{0:T(512)} %param.26) | copy-start | bytes 4612
  384.5 188.1 %copy-start.25 = (bf16[1,128,128]{2,1,0:T(8,128)(2,1)S(1)}, bf16[1,128,128]{2,1,0:T(8,128)(2,1)}, u32[]{:S(2)}) copy-start(bf16[1,128,128]{2,1,0:T(8,128)(2,1)} %param.29) | copy-start | bytes 98308
  385.3 208.0 %copy-start.13 = (bf16[360,128,2]{1,0,2:T(8,128)(2,1)}, bf16[360,128,2]{1,0,2:T(8,128)(2,1)S(1)}, u32[]{:S(2)}) copy-start(bf16[360,128,2]{1,0,2:T(8,128)(2,1)S(1)} %fusion.261) | copy-start | bytes 552964
  551.9 23.4 %copy-start.10 = (bf16[2,384,384]{2,1,0:T(8,128)(2,1)S(1)}, bf16[2,384,384]{2,1,0:T(8,128)(2,1)}, u32[]{:S(2)}) copy-start(bf16[2,384,384]{2,1,0:T(8,128)(2,1)} %param.31) | copy-start | bytes 1769476
  595.4 11.7 %copy-start.103 = (bf16[128]{0:T(256)(128)(2,1)S(1)}, bf16[128]{0:T(256)(128)(2,1)}, u32[]{:S(2)}) copy-start(bf16[128]{0:T(256)(128)(2,1)} %param.25) | copy-start | bytes 772
  602.3 13.7 %all-to-all-start.5 = ((bf16[64,2,1,2,384]{4,3,1,2,0:T(2,128)(2,1)}), bf16[64,2,1,2,384]{4,3,1,2,0:T(2,128)(2,1)S(1)}, u32[]{:S(2)}, u32[]{:S(2)}) async-start(bf16[64,2,1,2,384]{4,3,1,2,0:T(2,128)(2,1)} %copy.84), calls=%async_computation.5 | async-start | bytes 393216 | tf_op jit(solution)/shard_map/all_to_all | solution.py:27
  622.3 16.4 %all-to-all-start.6 = ((bf16[128,2,384]{2,1,0:T(2,128)(2,1)}), bf16[128,2,384]{2,1,0:T(2,128)(2,1)}, u32[]{:S(2)}, u32[]{:S(2)}) async-start(bf16[128,2,384]{2,1,0:T(2,128)(2,1)} %copy.87), calls=%async_computation.6 | async-start | bytes 393216 | tf_op jit(solution)/shard_map/all_to_all | solution.py:179
  628.5 22.9 %copy-start.29 = (bf16[384,8]{0,1:T(8,128)(2,1)S(1)}, bf16[384,8]{0,1:T(8,128)(2,1)}, u32[]{:S(2)}) copy-start(bf16[384,8]{0,1:T(8,128)(2,1)} %param.27) | copy-start | bytes 18436
  641.5 20.0 %all-to-all-start.7 = ((f32[128,1,360]{2,1,0:T(1,128)}), f32[128,1,360]{2,1,0:T(1,128)}, u32[]{:S(2)}, u32[]{:S(2)}) async-start(f32[128,1,360]{2,1,0:T(1,128)} %stack.26), calls=%async_computation.7 | async-start | bytes 393216 | tf_op jit(solution)/shard_map/all_to_all | solution.py:199
  (82 other events, 443.9 us)
Sparse Core Ops, SparseCore 0:
  384.6 163.4 all-reduce.4
